TPU v7x, 32 devices: a whole 2x2x4 slice. The times are simulated.
32 devices in a mesh: ctx: 8 (over z, x), head: 4 (over y, core).
Axes of the slice: x: 2, y: 2, z: 4, core: 2. Of those that a mesh axis runs over, the one named last changes fastest.
Arguments:
- queries: bfloat16 [2048, 2048], P(('ctx', 'head')), may hold values from -6 to 6
- key_vectors_state: bfloat16 [2048, 512], P(('ctx', 'head')), may hold values from -6 to 6
- value_vectors_state: bfloat16 [2048, 512], P(('ctx', 'head')), may hold values from -6 to 6
- doc_bounds: int32 [17], replicated, may hold values from 0 to 2048, as said below
Outputs:
- attended: bfloat16 [2048, 2048], P(('ctx', 'head'))
Inputs may be any that keep to these rules, and one draw needn't show every extreme that they name: doc_bounds[0] is 0 and doc_bounds[16] is 2048; the entries strictly increase, and doc_bounds[1] to doc_bounds[15] all lie below 1024, so the last document holds at least half of the tokens.
All inputs are finite; a program needn't handle non-finite values.
Results may differ from a plain program's by a relative error of at most 0.004.
Values may be sent and summed in bfloat16 or wider, within the bound.
A program may use at most 64 MiB of HBM per device.

v0:
```python
import math
import jax
import jax.numpy as jnp
from jax import lax
from jax.sharding import PartitionSpec as P

QUERY_HEADS = 32
KEY_VALUE_HEADS = 8
HEAD_SIZE = 64
masked_score = -1e30


def from_behind(block, axis, distance):
    devices = range(lax.axis_size(axis))
    route = [((i - distance) % len(devices), i) for i in devices]
    return lax.ppermute(block, axis, route)


def document_of(positions, doc_bounds):
    interior = doc_bounds[1:-1]
    return jnp.sum((interior[None, :] <= positions[:, None]).astype(jnp.int32), axis=1)


def on_device(queries, key_vectors_state, value_vectors_state, doc_bounds):
    query_loc, key_loc, value_loc = (
        lax.all_to_all(queries, "head", split_axis=1, concat_axis=0, tiled=True),
        lax.all_to_all(key_vectors_state, "head", split_axis=1, concat_axis=0, tiled=True),
        lax.all_to_all(value_vectors_state, "head", split_axis=1, concat_axis=0, tiled=True),
    )
    tok_rows = query_loc.shape[0]
    cycle_size = lax.axis_size("ctx")
    my_index = lax.axis_index("ctx")
    kv_local = key_loc.shape[1] // HEAD_SIZE
    queries_per_group = QUERY_HEADS // KEY_VALUE_HEADS
    score_scale = 1.0 / math.sqrt(HEAD_SIZE)
    first_pos = my_index * tok_rows
    query_pos = first_pos + jnp.arange(tok_rows, dtype=jnp.int32)
    heads_of_queries = query_loc.reshape(tok_rows, kv_local, queries_per_group, HEAD_SIZE)
    query_doc = document_of(query_pos, doc_bounds)

    def attend(running, key_piece, value_piece, anchor):
        key_count = key_piece.shape[0]
        key_pos = anchor + jnp.arange(key_count, dtype=jnp.int32)
        key_doc = document_of(key_pos, doc_bounds)
        allowed = (
            (query_doc[:, None] == key_doc[None, :])
            & (key_pos[None, :] <= query_pos[:, None])
            & (key_pos[None, :] >= 0)
        )
        heads_of_keys = key_piece.reshape(key_count, kv_local, HEAD_SIZE)
        heads_of_values = value_piece.reshape(key_count, kv_local, HEAD_SIZE)
        run_max, run_sum, weighted = running
        scores = (
            jnp.einsum(
                "qgjd,kgd->qgjk",
                heads_of_queries,
                heads_of_keys,
                preferred_element_type=jnp.float32,
            )
            * score_scale
        )
        visible = allowed[:, None, None, :]
        masked = jnp.where(visible, scores, masked_score)
        new_max = jnp.maximum(run_max, jnp.max(masked, axis=-1))
        weights = jnp.exp(masked - new_max[..., None]) * visible.astype(jnp.float32)
        shrink = jnp.exp(run_max - new_max)
        new_sum = run_sum * shrink + jnp.sum(weights, axis=-1)
        rounded = weights.astype(jnp.bfloat16)
        mixed = jnp.einsum(
            "qgjk,kgd->qgjd", rounded, heads_of_values, preferred_element_type=jnp.float32
        )
        return (new_max, new_sum, weighted * shrink[..., None] + mixed)

    def fold_keys(running, key_piece, value_piece, anchor):
        key_count = key_piece.shape[0]
        return attend(running, key_piece, value_piece, anchor)

    stat_shape = (tok_rows, kv_local, queries_per_group)
    initial = (
        jnp.full(stat_shape, masked_score, jnp.float32),
        jnp.zeros(stat_shape, jnp.float32),
        jnp.zeros((tok_rows, kv_local, queries_per_group, HEAD_SIZE), jnp.float32),
    )
    bound_heads = doc_bounds[:-1]
    doc_start = jnp.max(
        jnp.where(bound_heads[None, :] <= query_pos[:, None], bound_heads[None, :], 0), axis=1
    )
    start_block = doc_start // tok_rows
    own_block = query_pos // tok_rows
    row_turns = jnp.where(
        own_block <= my_index,
        my_index - start_block,
        jnp.where(start_block <= my_index, cycle_size - 1, my_index - start_block + cycle_size),
    )
    reach_steps = lax.pmax(jnp.max(row_turns), "ctx")
    running = fold_keys(initial, key_loc, value_loc, first_pos)

    def cycle_turn(turn_index, state):
        paired, inner_state = state
        paired = from_behind(paired, "ctx", 1)
        anchor = jnp.mod(my_index - turn_index - 1, cycle_size) * tok_rows
        return (paired, fold_keys(inner_state, paired[0], paired[1], anchor))

    stacked = jnp.stack((key_loc, value_loc))
    stacked, running = lax.fori_loop(0, reach_steps, cycle_turn, (stacked, running))
    run_max, run_sum, weighted = running
    attended = (
        (weighted / run_sum[..., None])
        .astype(jnp.bfloat16)
        .reshape(tok_rows, kv_local * queries_per_group * HEAD_SIZE)
    )
    return lax.all_to_all(attended, "head", split_axis=0, concat_axis=1, tiled=True)


def solution(mesh):
    return jax.shard_map(
        on_device,
        mesh=mesh,
        in_specs=(
            P(("ctx", "head"), None),
            P(("ctx", "head"), None),
            P(("ctx", "head"), None),
            P(),
        ),
        out_specs=P(("ctx", "head"), None),
        check_vma=False,
    )
```

profile of v0, /device:TPU:0, one launch (start us, length us, event | category | flops | bytes accessed | tf_op | source)
XLA Modules:
  0.0 87.6 jit_solution(5063558174066637305)
XLA Ops:
  0.0 0.8 copy-done
  0.8 0.6 copy_bitcast_fusion.2
  1.5 4.3 %all-to-all-start = ((bf16[64,4,128]{2,0,1:T(8,128)(2,1)}), bf16[64,4,128]{2,0,1:T(8,128)(2,1)S(1)}, u32[]{:S(2)}, u32[]{:S(2)}) async-start(bf16[64,4,128]{2,0,1:T(8,128)(2,1)} %copy_bitcast_fusion.2), calls=%async_computation | async-start | bytes 131072 | tf_op jit(solution)/shard_map/all_to_all | solution.py:27
  5.7 0.7 slice.25
  6.6 0.7 select_reduce_fusion
  7.3 1.5 %copy_bitcast_fusion.1 = bf16[64,4,128]{2,0,1:T(8,128)(2,1)} fusion(bf16[64,512]{1,0:T(8,128)(2,1)} %param.8), kind=kLoop, calls=%fused_computation.40 | loop fusion | bytes 131072 | tf_op jit(solution)/shard_map/all_to_all | solution.py:28
  9.9 3.3 %all-to-all-start.1 = ((bf16[64,4,128]{2,0,1:T(8,128)(2,1)}), bf16[64,4,128]{2,0,1:T(8,128)(2,1)S(1)}, u32[]{:S(2)}, u32[]{:S(2)}) async-start(bf16[64,4,128]{2,0,1:T(8,128)(2,1)} %copy_bitcast_fusion.1), calls=%async_computation.1 | async-start | bytes 131072 | tf_op jit(solution)/shard_map/all_to_all | solution.py:28
  13.2 1.7 %copy.82 = bf16[8,4,8,512]{3,2,0,1:T(8,128)(2,1)} copy(bf16[8,4,8,512]{3,2,1,0:T(8,128)(2,1)} %bitcast.126) | data formatting | bytes 524288 | tf_op jit(solution)/shard_map/all_to_all | solution.py:26
  14.8 2.4 %all-to-all-done.1 = bf16[64,4,128]{2,0,1:T(8,128)(2,1)S(1)} async-done(((bf16[64,4,128]{2,0,1:T(8,128)(2,1)}), bf16[64,4,128]{2,0,1:T(8,128)(2,1)S(1)}, u32[]{:S(2)}, u32[]{:S(2)}) %all-to-all-start.1) | async-done | bytes 65568 | tf_op jit(solution)/shard_map/all_to_all | solution.py:28
  17.2 3.4 %all-to-all-start.2 = ((bf16[64,4,512]{2,0,1:T(8,128)(2,1)}), bf16[64,4,512]{2,0,1:T(8,128)(2,1)S(1)}, u32[]{:S(2)}, u32[]{:S(2)}) async-start(bf16[64,4,512]{2,0,1:T(8,128)(2,1)} %bitcast.73), calls=%async_computation.2 | async-start | bytes 524288 | tf_op jit(solution)/shard_map/all_to_all | solution.py:26
  20.8 12.6 %pmax.7 = s32[]{:T(128)} all-reduce(s32[]{:T(128)} %fusion.26), channel_id=1, replica_groups=mesh['ctx'=8,'head'=4] {'ctx'}, use_global_device_ids=true, to_apply=%region_5.6 | all-reduce | flops 1 | bytes 8 | tf_op jit(solution)/shard_map/pmax | solution.py:95
  35.4 0.7 fusion.17
  36.2 41.1 %while.19 = (s32[]{:T(128)}, bf16[2,256,128]{1,2,0:T(8,128)(2,1)S(1)}, f32[256,2,4]{0,2,1:T(4,128)S(1)}, f32[256,2,4]{0,2,1:T(4,128)S(1)}, f32[256,2,4,64]{0,3,2...) while((s32[]{:T(128)}, ...), condition=%wide.region_10.11_spmd.clone, body=%wide.region_6.10_spmd.clone.sunk | while | flops 141639696 | bytes 9970710 | solution.py:105
  36.7 1.5 %collective-permute-start = (bf16[2,256,128]{1,2,0:T(8,128)(2,1)S(1)}, bf16[2,256,128]{1,2,0:T(8,128)(2,1)S(1)}, u32[]{:S(2)}, u32[]{:S(2)}) collective-permute-start(bf16[2,256,128]{1,2,0:T(8,128)(2,1)S(1)} %get-tuple-element.362), channel_id=1, source_target_pairs={{28,0},{0,4},{4,8},{8,12},{12,16},{16,20},{20,24},{24,28},{29,1},{... | collective-permute-start | bytes 393224 | tf_op jit(solution)/shard_map/while/body/ppermute | solution.py:16
  38.7 5.8 %collective-permute-done = bf16[2,256,128]{1,2,0:T(8,128)(2,1)S(1)} collective-permute-done((bf16[2,256,128]{1,2,0:T(8,128)(2,1)S(1)}, bf16[2,256,128]{1,2,0:T(8,128)(2,1)S(1)}, u32[]{:S(2)}, u32[]{:S(2)}) %collective-permute-start) | collective-permute-done | bytes 131104 | tf_op jit(solution)/shard_map/while/body/ppermute | solution.py:16
  45.5 0.7 fusion.56
  47.3 7.3 %collective-permute-done = bf16[2,256,128]{1,2,0:T(8,128)(2,1)S(1)} collective-permute-done((bf16[2,256,128]{1,2,0:T(8,128)(2,1)S(1)}, bf16[2,256,128]{1,2,0:T(8,128)(2,1)S(1)}, u32[]{:S(2)}, u32[]{:S(2)}) %collective-permute-start) | collective-permute-done | bytes 131104 | tf_op jit(solution)/shard_map/while/body/ppermute | solution.py:16
  55.7 0.7 fusion.56
  57.5 7.3 %collective-permute-done = bf16[2,256,128]{1,2,0:T(8,128)(2,1)S(1)} collective-permute-done((bf16[2,256,128]{1,2,0:T(8,128)(2,1)S(1)}, bf16[2,256,128]{1,2,0:T(8,128)(2,1)S(1)}, u32[]{:S(2)}, u32[]{:S(2)}) %collective-permute-start) | collective-permute-done | bytes 131104 | tf_op jit(solution)/shard_map/while/body/ppermute | solution.py:16
  65.8 0.7 fusion.56
  67.6 7.3 %collective-permute-done = bf16[2,256,128]{1,2,0:T(8,128)(2,1)S(1)} collective-permute-done((bf16[2,256,128]{1,2,0:T(8,128)(2,1)S(1)}, bf16[2,256,128]{1,2,0:T(8,128)(2,1)S(1)}, u32[]{:S(2)}, u32[]{:S(2)}) %collective-permute-start) | collective-permute-done | bytes 131104 | tf_op jit(solution)/shard_map/while/body/ppermute | solution.py:16
  75.9 0.7 fusion.56
  77.9 9.1 %all_to_all.67 = bf16[4,64,512]{2,1,0:T(8,128)(2,1)S(1)} all-to-all(bf16[4,64,512]{2,1,0:T(8,128)(2,1)S(1)} %copy.68), channel_id=1, replica_groups=mesh['ctx'=8,'head'=4] {'head'}, dimensions={0} | all-to-all | bytes 524288 | tf_op jit(solution)/shard_map/all_to_all | solution.py:112
  86.9 0.7 copy.72
  (78 shorter events, 9.7 us)
Async XLA Ops:
  0.0 0.8 copy-start
  1.5 8.4 %all-to-all-start = ((bf16[64,4,128]{2,0,1:T(8,128)(2,1)}), bf16[64,4,128]{2,0,1:T(8,128)(2,1)S(1)}, u32[]{:S(2)}, u32[]{:S(2)}) async-start(bf16[64,4,128]{2,0,1:T(8,128)(2,1)} %copy_bitcast_fusion.2), calls=%async_computation | async-start | bytes 131072 | tf_op jit(solution)/shard_map/all_to_all | solution.py:27
  9.9 7.4 %all-to-all-start.1 = ((bf16[64,4,128]{2,0,1:T(8,128)(2,1)}), bf16[64,4,128]{2,0,1:T(8,128)(2,1)S(1)}, u32[]{:S(2)}, u32[]{:S(2)}) async-start(bf16[64,4,128]{2,0,1:T(8,128)(2,1)} %copy_bitcast_fusion.1), calls=%async_computation.1 | async-start | bytes 131072 | tf_op jit(solution)/shard_map/all_to_all | solution.py:28
  17.2 16.5 %all-to-all-start.2 = ((bf16[64,4,512]{2,0,1:T(8,128)(2,1)}), bf16[64,4,512]{2,0,1:T(8,128)(2,1)S(1)}, u32[]{:S(2)}, u32[]{:S(2)}) async-start(bf16[64,4,512]{2,0,1:T(8,128)(2,1)} %bitcast.73), calls=%async_computation.2 | async-start | bytes 524288 | tf_op jit(solution)/shard_map/all_to_all | solution.py:26
  35.4 0.8 copy-start.1
  36.7 7.7 %collective-permute-start = (bf16[2,256,128]{1,2,0:T(8,128)(2,1)S(1)}, bf16[2,256,128]{1,2,0:T(8,128)(2,1)S(1)}, u32[]{:S(2)}, u32[]{:S(2)}) collective-permute-start(bf16[2,256,128]{1,2,0:T(8,128)(2,1)S(1)} %get-tuple-element.362), channel_id=1, source_target_pairs={{28,0},{0,4},{4,8},{8,12},{12,16},{16,20},{20,24},{24,28},{29,1},{... | collective-permute-start | bytes 393224 | tf_op jit(solution)/shard_map/while/body/ppermute | solution.py:16
  46.9 7.7 %collective-permute-start = (bf16[2,256,128]{1,2,0:T(8,128)(2,1)S(1)}, bf16[2,256,128]{1,2,0:T(8,128)(2,1)S(1)}, u32[]{:S(2)}, u32[]{:S(2)}) collective-permute-start(bf16[2,256,128]{1,2,0:T(8,128)(2,1)S(1)} %get-tuple-element.362), channel_id=1, source_target_pairs={{28,0},{0,4},{4,8},{8,12},{12,16},{16,20},{20,24},{24,28},{29,1},{... | collective-permute-start | bytes 393224 | tf_op jit(solution)/shard_map/while/body/ppermute | solution.py:16
  57.0 7.7 %collective-permute-start = (bf16[2,256,128]{1,2,0:T(8,128)(2,1)S(1)}, bf16[2,256,128]{1,2,0:T(8,128)(2,1)S(1)}, u32[]{:S(2)}, u32[]{:S(2)}) collective-permute-start(bf16[2,256,128]{1,2,0:T(8,128)(2,1)S(1)} %get-tuple-element.362), channel_id=1, source_target_pairs={{28,0},{0,4},{4,8},{8,12},{12,16},{16,20},{20,24},{24,28},{29,1},{... | collective-permute-start | bytes 393224 | tf_op jit(solution)/shard_map/while/body/ppermute | solution.py:16
  67.1 7.7 %collective-permute-start = (bf16[2,256,128]{1,2,0:T(8,128)(2,1)S(1)}, bf16[2,256,128]{1,2,0:T(8,128)(2,1)S(1)}, u32[]{:S(2)}, u32[]{:S(2)}) collective-permute-start(bf16[2,256,128]{1,2,0:T(8,128)(2,1)S(1)} %get-tuple-element.362), channel_id=1, source_target_pairs={{28,0},{0,4},{4,8},{8,12},{12,16},{16,20},{20,24},{24,28},{29,1},{... | collective-permute-start | bytes 393224 | tf_op jit(solution)/shard_map/while/body/ppermute | solution.py:16
where the time goes:
time: 88.2 us; the launch traced here: 87.6 us
  waiting for transfers between devices  30.4 us (34%)
  blocking collectives  21.7 us (25%)
  starting transfers between devices  12.7 us (14%)
  local copies, waits for them, and re-layouts  7.91 us (9%)
  matrix products  6.12 us (7%)
  other arithmetic  5.49 us (6%)
  loops' own time  3.19 us (4%)
    ppermute x4, waiting for transfers between devices, from_behind(): return lax.ppermute(block, axis, route)  27.6 us
    pmax x1, blocking collectives, on_device(): reach_steps = lax.pmax(jnp.max(row_turns), 'ctx')  12.6 us
    all_to_all x1, blocking collectives, on_device(): lax.all_to_all(attended, 'head', split_axis=0, concat_axis=1, tiled=True)  9.06 us
    all_to_all x1, starting transfers between devices, on_device(): lax.all_to_all(key_vectors_state, 'head', split_axis=1, concat_axis=0, ti...  4.26 us
    dot_general x5, matrix products, attend(): jnp.einsum('qgjk,kgd->qgjd', rounded, heads_of_values, preferred_element_...  3.68 us
    all_to_all x1, starting transfers between devices, on_device(): lax.all_to_all(queries, 'head', split_axis=1, concat_axis=0, tiled=True)  3.41 us
    all_to_all x1, starting transfers between devices, on_device(): lax.all_to_all(value_vectors_state, 'head', split_axis=1, concat_axis=0,...  3.28 us
    another operation x1, loops' own time, on_device(): lax.fori_loop(0, reach_steps, cycle_turn, (stacked, running))  3.19 us
  transfers between devices with their start and end apart: 7, of which 6 were waited for; matrix products, arithmetic and copies ran while one was open for 8% of the time, Pallas kernels for 0%

commit v1 on v0

--- a/solution.py
+++ b/solution.py
@@ -8,6 +8,23 @@
 KEY_VALUE_HEADS = 8
 HEAD_SIZE = 64
 masked_score = -1e30
+
+
+def connect_vector(inner_x, d_out, axis_no):
+    dev_axis = "head"
+    q_next, arr_out = (jax.lax.axis_size(dev_axis), jax.lax.axis_index(dev_axis))
+    answer = inner_x.shape[d_out] // q_next
+    newest = jnp.roll(inner_x, -arr_out * answer, d_out)
+    log = [lax.slice_in_dim(newest, 0, answer, axis=d_out)]
+    k0 = 1
+    while k0 < q_next:
+        main = lax.slice_in_dim(newest, k0 * answer, (k0 + 1) * answer, axis=d_out)
+        log.append(
+            jax.lax.ppermute(main, dev_axis, [(d, (d + k0) % q_next) for d in range(q_next)])
+        )
+        k0 += 1
+    work_now = jnp.concatenate(log[::-1], axis_no)
+    return jnp.roll(work_now, (arr_out + 1) * log[0].shape[axis_no], axis_no)
 
 
 def from_behind(block, axis, distance):
@@ -23,7 +40,7 @@
 
 def on_device(queries, key_vectors_state, value_vectors_state, doc_bounds):
     query_loc, key_loc, value_loc = (
-        lax.all_to_all(queries, "head", split_axis=1, concat_axis=0, tiled=True),
+        connect_vector(queries, 1, 0),
         lax.all_to_all(key_vectors_state, "head", split_axis=1, concat_axis=0, tiled=True),
         lax.all_to_all(value_vectors_state, "head", split_axis=1, concat_axis=0, tiled=True),
     )

time: 88.2 us -> 84.6 us (0.959)
  waiting for transfers between devices: 30.4 us -> 27.6 us
  local copies, waits for them, and re-layouts: 7.91 us -> 5.86 us
  other arithmetic: 5.49 us -> 6.55 us
    ppermute x0 -> x3, starting transfers between devices: none -> 3.58 us  [connect_vector(): jax.lax.ppermute(main, dev_axis, [(d, (d + k0) % q_next) for d in range(q...]
    all_to_all x1 -> x0, starting transfers between devices: 3.41 us -> none  [on_device(): lax.all_to_all(queries, 'head', split_axis=1, concat_axis=0, tiled=True)]
    all_to_all x1, waiting for transfers between devices: 2.4 us -> 0.01 us  [on_device(): lax.all_to_all(value_vectors_state, 'head', split_axis=1, concat_axis=0,...]
    all_to_all x1 -> x0, local copies, waits for them, and re-layouts: 1.68 us -> none  [on_device(): lax.all_to_all(queries, 'head', split_axis=1, concat_axis=0, tiled=True)]
    concatenate x0 -> x1, other arithmetic: none -> 1.06 us  [connect_vector(): newest = jnp.roll(inner_x, -arr_out * answer, d_out)]
    all_to_all x1, starting transfers between devices: 3.28 us -> 4.26 us  [on_device(): lax.all_to_all(value_vectors_state, 'head', split_axis=1, concat_axis=0,...]
    all_to_all x1, starting transfers between devices: 4.26 us -> 3.29 us  [on_device(): lax.all_to_all(key_vectors_state, 'head', split_axis=1, concat_axis=0, ti...]
  transfers between devices with their start and end apart: 7 -> 9, of which waited for: 6 -> 4; matrix products, arithmetic and copies ran while one was open for 8% -> 8% of each run, Pallas kernels for 0% -> 0%
where the time goes in v1:
time: 84.6 us; the launch traced here: 84.1 us
  waiting for transfers between devices  27.6 us (33%)
  blocking collectives  21.6 us (26%)
  starting transfers between devices  12.9 us (15%)
  other arithmetic  6.55 us (8%)
  matrix products  6.12 us (7%)
  local copies, waits for them, and re-layouts  5.86 us (7%)
  loops' own time  3.19 us (4%)
    ppermute x4, waiting for transfers between devices, from_behind(): return lax.ppermute(block, axis, route)  27.6 us
    pmax x1, blocking collectives, on_device(): reach_steps = lax.pmax(jnp.max(row_turns), 'ctx')  12.6 us
    all_to_all x1, blocking collectives, on_device(): lax.all_to_all(attended, 'head', split_axis=0, concat_axis=1, tiled=True)  9.06 us
    all_to_all x1, starting transfers between devices, on_device(): lax.all_to_all(value_vectors_state, 'head', split_axis=1, concat_axis=0,...  4.26 us
    dot_general x5, matrix products, attend(): jnp.einsum('qgjk,kgd->qgjd', rounded, heads_of_values, preferred_element_...  3.68 us
    ppermute x3, starting transfers between devices, connect_vector(): jax.lax.ppermute(main, dev_axis, [(d, (d + k0) % q_next) for d in range(q...  3.58 us
    all_to_all x1, starting transfers between devices, on_device(): lax.all_to_all(key_vectors_state, 'head', split_axis=1, concat_axis=0, ti...  3.29 us
    another operation x1, loops' own time, on_device(): lax.fori_loop(0, reach_steps, cycle_turn, (stacked, running))  3.19 us
  transfers between devices with their start and end apart: 9, of which 4 were waited for; matrix products, arithmetic and copies ran while one was open for 8% of the time, Pallas kernels for 0%

profile of v1, /device:TPU:0, one launch (start us, length us, event | category | flops | bytes accessed | tf_op | source)
XLA Modules:
  0.0 84.1 jit_solution(15840380650065122728)
XLA Ops:
  0.0 0.8 copy-done
  0.8 0.6 copy_bitcast_fusion
  1.5 4.3 %all-to-all-start.1 = ((bf16[64,4,128]{2,0,1:T(8,128)(2,1)}), bf16[64,4,128]{2,0,1:T(8,128)(2,1)S(1)}, u32[]{:S(2)}, u32[]{:S(2)}) async-start(bf16[64,4,128]{2,0,1:T(8,128)(2,1)} %copy_bitcast_fusion), calls=%async_computation.1 | async-start | bytes 131072 | tf_op jit(solution)/shard_map/all_to_all | solution.py:45
  5.7 1.1 %fusion.24 = bf16[64,2048]{1,0:T(8,128)(2,1)S(1)} fusion(s32[]{:T(128)S(6)} %select_n.69, bf16[64,2048]{1,0:T(8,128)(2,1)} %param.6), kind=kLoop, calls=%fused_computation.38 | loop fusion | flops 524288 | bytes 524292 | tf_op jit(solution)/shard_map/jit(_roll_dynamic)/concatenate | solution.py:17
  7.4 1.7 %collective-permute-start.2 = (bf16[64,512]{1,0:T(8,128)(2,1)S(1)}, bf16[64,512]{1,0:T(8,128)(2,1)S(1)}, u32[]{:S(2)}, u32[]{:S(2)}) collective-permute-start(bf16[64,512]{1,0:T(8,128)(2,1)S(1)} %get-tuple-element.251), channel_id=1, source_target_pairs={{0,2},{1,3},{2,0},{3,1},{4,6},{5,7},{6,4},{7,5},{8,10},{9,11},{10,... | collective-permute-start | bytes 196616 | tf_op jit(solution)/shard_map/ppermute | solution.py:23
  9.0 1.4 %collective-permute-start.1 = (bf16[64,512]{1,0:T(8,128)(2,1)S(1)}, bf16[64,512]{1,0:T(8,128)(2,1)S(1)}, u32[]{:S(2)}, u32[]{:S(2)}) collective-permute-start(bf16[64,512]{1,0:T(8,128)(2,1)S(1)} %get-tuple-element.252), channel_id=1, source_target_pairs={{0,3},{1,0},{2,1},{3,2},{4,7},{5,4},{6,5},{7,6},{8,11},{9,8},{10,9... | collective-permute-start | bytes 196616 | tf_op jit(solution)/shard_map/ppermute | solution.py:23
  10.4 0.7 slice.37
  11.2 0.7 select_reduce_fusion
  12.6 1.5 %copy_bitcast_fusion.1 = bf16[64,4,128]{2,0,1:T(8,128)(2,1)} fusion(bf16[64,512]{1,0:T(8,128)(2,1)} %param.7), kind=kLoop, calls=%fused_computation.45 | loop fusion | bytes 131072 | tf_op jit(solution)/shard_map/all_to_all | solution.py:44
  14.1 3.3 %all-to-all-start = ((bf16[64,4,128]{2,0,1:T(8,128)(2,1)}), bf16[64,4,128]{2,0,1:T(8,128)(2,1)S(1)}, u32[]{:S(2)}, u32[]{:S(2)}) async-start(bf16[64,4,128]{2,0,1:T(8,128)(2,1)} %copy_bitcast_fusion.1), calls=%async_computation | async-start | bytes 131072 | tf_op jit(solution)/shard_map/all_to_all | solution.py:44
  17.6 12.6 %pmax.7 = s32[]{:T(128)} all-reduce(s32[]{:T(128)} %fusion.28), channel_id=1, replica_groups=mesh['ctx'=8,'head'=4] {'ctx'}, use_global_device_ids=true, to_apply=%region_5.6 | all-reduce | flops 1 | bytes 8 | tf_op jit(solution)/shard_map/pmax | solution.py:112
  31.8 0.7 fusion.18
  32.6 41.1 %while.19 = (s32[]{:T(128)}, bf16[2,256,128]{1,2,0:T(8,128)(2,1)S(1)}, f32[256,2,4]{0,2,1:T(4,128)S(1)}, f32[256,2,4]{0,2,1:T(4,128)S(1)}, f32[256,2,4,64]{0,3,2...) while((s32[]{:T(128)}, ...), condition=%wide.region_10.11_spmd.clone, body=%wide.region_6.10_spmd.clone.sunk | while | flops 141639696 | bytes 9970710 | solution.py:122
  33.2 1.6 %collective-permute-start = (bf16[2,256,128]{1,2,0:T(8,128)(2,1)S(1)}, bf16[2,256,128]{1,2,0:T(8,128)(2,1)S(1)}, u32[]{:S(2)}, u32[]{:S(2)}) collective-permute-start(bf16[2,256,128]{1,2,0:T(8,128)(2,1)S(1)} %get-tuple-element.365), channel_id=1, source_target_pairs={{28,0},{0,4},{4,8},{8,12},{12,16},{16,20},{20,24},{24,28},{29,1},{... | collective-permute-start | bytes 393224 | tf_op jit(solution)/shard_map/while/body/ppermute | solution.py:33
  35.1 5.8 %collective-permute-done = bf16[2,256,128]{1,2,0:T(8,128)(2,1)S(1)} collective-permute-done((bf16[2,256,128]{1,2,0:T(8,128)(2,1)S(1)}, bf16[2,256,128]{1,2,0:T(8,128)(2,1)S(1)}, u32[]{:S(2)}, u32[]{:S(2)}) %collective-permute-start) | collective-permute-done | bytes 131104 | tf_op jit(solution)/shard_map/while/body/ppermute | solution.py:33
  42.0 0.7 fusion.59
  43.7 7.3 %collective-permute-done = bf16[2,256,128]{1,2,0:T(8,128)(2,1)S(1)} collective-permute-done((bf16[2,256,128]{1,2,0:T(8,128)(2,1)S(1)}, bf16[2,256,128]{1,2,0:T(8,128)(2,1)S(1)}, u32[]{:S(2)}, u32[]{:S(2)}) %collective-permute-start) | collective-permute-done | bytes 131104 | tf_op jit(solution)/shard_map/while/body/ppermute | solution.py:33
  52.1 0.7 fusion.59
  53.9 7.3 %collective-permute-done = bf16[2,256,128]{1,2,0:T(8,128)(2,1)S(1)} collective-permute-done((bf16[2,256,128]{1,2,0:T(8,128)(2,1)S(1)}, bf16[2,256,128]{1,2,0:T(8,128)(2,1)S(1)}, u32[]{:S(2)}, u32[]{:S(2)}) %collective-permute-start) | collective-permute-done | bytes 131104 | tf_op jit(solution)/shard_map/while/body/ppermute | solution.py:33
  62.2 0.7 fusion.59
  64.0 7.3 %collective-permute-done = bf16[2,256,128]{1,2,0:T(8,128)(2,1)S(1)} collective-permute-done((bf16[2,256,128]{1,2,0:T(8,128)(2,1)S(1)}, bf16[2,256,128]{1,2,0:T(8,128)(2,1)S(1)}, u32[]{:S(2)}, u32[]{:S(2)}) %collective-permute-start) | collective-permute-done | bytes 131104 | tf_op jit(solution)/shard_map/while/body/ppermute | solution.py:33
  72.3 0.7 fusion.59
  74.3 9.1 %all_to_all.51 = bf16[4,64,512]{2,1,0:T(8,128)(2,1)S(1)} all-to-all(bf16[4,64,512]{2,1,0:T(8,128)(2,1)S(1)} %copy.60), channel_id=1, replica_groups=mesh['ctx'=8,'head'=4] {'head'}, dimensions={0} | all-to-all | bytes 524288 | tf_op jit(solution)/shard_map/all_to_all | solution.py:129
  83.3 0.7 copy.63
  (91 shorter events, 9.4 us)
Async XLA Ops:
  0.0 0.8 copy-start
  1.5 12.6 %all-to-all-start.1 = ((bf16[64,4,128]{2,0,1:T(8,128)(2,1)}), bf16[64,4,128]{2,0,1:T(8,128)(2,1)S(1)}, u32[]{:S(2)}, u32[]{:S(2)}) async-start(bf16[64,4,128]{2,0,1:T(8,128)(2,1)} %copy_bitcast_fusion), calls=%async_computation.1 | async-start | bytes 131072 | tf_op jit(solution)/shard_map/all_to_all | solution.py:45
  6.8 23.7 %collective-permute-start.3 = (bf16[64,512]{1,0:T(8,128)(2,1)S(1)}, bf16[64,512]{1,0:T(8,128)(2,1)S(1)}, u32[]{:S(2)}, u32[]{:S(2)}) collective-permute-start(bf16[64,512]{1,0:T(8,128)(2,1)S(1)} %get-tuple-element.250), channel_id=1, source_target_pairs={{0,1},{1,2},{2,3},{3,0},{4,5},{5,6},{6,7},{7,4},{8,9},{9,10},{10,1... | collective-permute-start | bytes 196616 | tf_op jit(solution)/shard_map/ppermute | solution.py:23
  7.4 23.2 %collective-permute-start.2 = (bf16[64,512]{1,0:T(8,128)(2,1)S(1)}, bf16[64,512]{1,0:T(8,128)(2,1)S(1)}, u32[]{:S(2)}, u32[]{:S(2)}) collective-permute-start(bf16[64,512]{1,0:T(8,128)(2,1)S(1)} %get-tuple-element.251), channel_id=1, source_target_pairs={{0,2},{1,3},{2,0},{3,1},{4,6},{5,7},{6,4},{7,5},{8,10},{9,11},{10,... | collective-permute-start | bytes 196616 | tf_op jit(solution)/shard_map/ppermute | solution.py:23
  9.0 21.5 %collective-permute-start.1 = (bf16[64,512]{1,0:T(8,128)(2,1)S(1)}, bf16[64,512]{1,0:T(8,128)(2,1)S(1)}, u32[]{:S(2)}, u32[]{:S(2)}) collective-permute-start(bf16[64,512]{1,0:T(8,128)(2,1)S(1)} %get-tuple-element.252), channel_id=1, source_target_pairs={{0,3},{1,0},{2,1},{3,2},{4,7},{5,4},{6,5},{7,6},{8,11},{9,8},{10,9... | collective-permute-start | bytes 196616 | tf_op jit(solution)/shard_map/ppermute | solution.py:23
  14.1 16.2 %all-to-all-start = ((bf16[64,4,128]{2,0,1:T(8,128)(2,1)}), bf16[64,4,128]{2,0,1:T(8,128)(2,1)S(1)}, u32[]{:S(2)}, u32[]{:S(2)}) async-start(bf16[64,4,128]{2,0,1:T(8,128)(2,1)} %copy_bitcast_fusion.1), calls=%async_computation | async-start | bytes 131072 | tf_op jit(solution)/shard_map/all_to_all | solution.py:44
  31.8 0.8 copy-start.1
  33.2 7.7 %collective-permute-start = (bf16[2,256,128]{1,2,0:T(8,128)(2,1)S(1)}, bf16[2,256,128]{1,2,0:T(8,128)(2,1)S(1)}, u32[]{:S(2)}, u32[]{:S(2)}) collective-permute-start(bf16[2,256,128]{1,2,0:T(8,128)(2,1)S(1)} %get-tuple-element.365), channel_id=1, source_target_pairs={{28,0},{0,4},{4,8},{8,12},{12,16},{16,20},{20,24},{24,28},{29,1},{... | collective-permute-start | bytes 393224 | tf_op jit(solution)/shard_map/while/body/ppermute | solution.py:33
  43.3 7.7 %collective-permute-start = (bf16[2,256,128]{1,2,0:T(8,128)(2,1)S(1)}, bf16[2,256,128]{1,2,0:T(8,128)(2,1)S(1)}, u32[]{:S(2)}, u32[]{:S(2)}) collective-permute-start(bf16[2,256,128]{1,2,0:T(8,128)(2,1)S(1)} %get-tuple-element.365), channel_id=1, source_target_pairs={{28,0},{0,4},{4,8},{8,12},{12,16},{16,20},{20,24},{24,28},{29,1},{... | collective-permute-start | bytes 393224 | tf_op jit(solution)/shard_map/while/body/ppermute | solution.py:33
  53.4 7.7 %collective-permute-start = (bf16[2,256,128]{1,2,0:T(8,128)(2,1)S(1)}, bf16[2,256,128]{1,2,0:T(8,128)(2,1)S(1)}, u32[]{:S(2)}, u32[]{:S(2)}) collective-permute-start(bf16[2,256,128]{1,2,0:T(8,128)(2,1)S(1)} %get-tuple-element.365), channel_id=1, source_target_pairs={{28,0},{0,4},{4,8},{8,12},{12,16},{16,20},{20,24},{24,28},{29,1},{... | collective-permute-start | bytes 393224 | tf_op jit(solution)/shard_map/while/body/ppermute | solution.py:33
  63.5 7.7 %collective-permute-start = (bf16[2,256,128]{1,2,0:T(8,128)(2,1)S(1)}, bf16[2,256,128]{1,2,0:T(8,128)(2,1)S(1)}, u32[]{:S(2)}, u32[]{:S(2)}) collective-permute-start(bf16[2,256,128]{1,2,0:T(8,128)(2,1)S(1)} %get-tuple-element.365), channel_id=1, source_target_pairs={{28,0},{0,4},{4,8},{8,12},{12,16},{16,20},{20,24},{24,28},{29,1},{... | collective-permute-start | bytes 393224 | tf_op jit(solution)/shard_map/while/body/ppermute | solution.py:33
